TPU v7x, 32 devices: a whole 2x2x4 slice. The times are simulated.
32 devices in a mesh: grp: 2 (over y), mode: 8 (over z, x), node: 2 (over core).
Axes of the slice: x: 2, y: 2, z: 4, core: 2. Of those that a mesh axis runs over, the one named last changes fastest.
Arguments:
- mode_basis: float32 [4096, 4096], P('mode', 'node'), may hold values from -6 to 6
- mode_scales: float32 [4096], P('mode'), may hold values from 0.003 to 0.02
- mean_log: float32 [4096], P(('node', 'mode')), may hold values from -0.5 to 0.5
- sample_seeds: int32 [4096], P('grp'), parts along dimension 0, may hold values from 0 to 1073741823
Outputs:
- modulus: float32 [4096, 4096], P(('node', 'mode'), 'grp'), parts along dimension 1
- sample_means: float32 [4096], P('grp'), parts along dimension 0
There are 2 independent parts, one for each index of `grp`. A program takes and returns all parts, laid end to end along the dimension named above; an argument that names none is the same for every part. Nothing has to cross between parts.
All inputs are finite; a program needn't handle non-finite values.
Results may differ from a plain program's by a relative error of at most 0.00005.
Values sent between devices are 32-bit elements; how exact they have to be, the bound alone decides.
No kernel may reach another device: no remote copies, remote signals or barrier semaphores. Data moves between devices by JAX's collectives and lax.ppermute only.
A program may use at most 64 MiB of HBM per device.

v0:
```python
import math
import jax
import jax.numpy as jnp
from jax import lax
from jax.sharding import PartitionSpec as P


def scramble(seed_words, counter_words):
    mixed_word = seed_words * -1640531527 + counter_words * 668265261
    mixed_word = mixed_word ^ mixed_word >> 15 & 131071
    mixed_word = mixed_word * -2048144789
    mixed_word = mixed_word ^ mixed_word >> 13 & 524287
    mixed_word = mixed_word * -1028477387
    mixed_word = mixed_word ^ mixed_word >> 16 & 65535
    return mixed_word


def normals(sample_seeds, mode_start, mode_count):
    mode_ids = mode_start + jnp.arange(mode_count, dtype=jnp.int32)
    seed_words = sample_seeds[None, :]
    counter_words = (2 * mode_ids)[:, None]
    first_word = scramble(seed_words, counter_words)
    second_word = scramble(seed_words, counter_words + 1)
    first_unit = ((first_word & 16777215).astype(jnp.float32) + 0.5) * (1.0 / 16777216.0)
    second_unit = ((second_word & 16777215).astype(jnp.float32) + 0.5) * (1.0 / 16777216.0)
    radius = jnp.sqrt(-2.0 * jnp.log(first_unit))
    return radius * jnp.cos(2.0 * math.pi * second_unit)


def contract_all(all_modes, sample_seeds):
    mode_total = all_modes.shape[0]
    block_modes = min(512, mode_total)
    block_count = mode_total // block_modes
    start_total = jnp.zeros((all_modes.shape[1], sample_seeds.shape[0]), jnp.float32)

    def add_block(block, total):
        first_mode = (block * block_modes).astype(jnp.int32)
        rows = lax.dynamic_slice_in_dim(all_modes, first_mode, block_modes, 0)
        coeffs = normals(sample_seeds, first_mode, block_modes)
        return total + lax.dot_general(
            rows,
            coeffs,
            (((0,), (0,)), ((), ())),
            precision=lax.Precision.HIGHEST,
            preferred_element_type=jnp.float32,
        )

    return lax.fori_loop(0, block_count, add_block, start_total)


def on_device(mode_basis, mode_scales, mean_log, sample_seeds):
    own_rows = mean_log.shape[0]
    scaled = mode_scales[:, None] * mode_basis
    gathered = lax.all_to_all(scaled, "mode", split_axis=1, concat_axis=0, tiled=True)
    summed = contract_all(gathered, sample_seeds)
    modulus = jnp.exp(mean_log[:, None] + summed)
    totals = lax.psum(jnp.sum(modulus, axis=0), ("mode", "node"))
    node_count = own_rows * lax.axis_size("mode") * lax.axis_size("node")
    return (modulus, totals / node_count)


def solution(mesh):
    return jax.shard_map(
        on_device,
        mesh=mesh,
        in_specs=(P("mode", "node"), P("mode"), P(("node", "mode")), P("grp")),
        out_specs=(P(("node", "mode"), "grp"), P("grp")),
        check_vma=False,
    )
```

profile of v0, /device:TPU:0, one launch (start us, length us, event | category | flops | bytes accessed | tf_op | source)
XLA Modules:
  0.0 334.7 jit_solution(1991284625481277206)
XLA Ops:
  0.6 2.5 broadcast_multiply_fusion.1
  3.2 2.4 copy.9
  5.5 0.0 copy-start
  5.5 7.4 %all-to-all-start = ((f32[512,8,256]{2,0,1:T(8,128)}), f32[512,8,256]{2,0,1:T(8,128)}, u32[]{:S(2)}, u32[]{:S(2)}) async-start(f32[512,8,256]{2,0,1:T(8,128)} %bitcast.8), calls=%async_computation | async-start | bytes 8388608 | tf_op jit(solution)/shard_map/all_to_all | solution.py:54
  12.9 93.3 %all-to-all-done = f32[512,8,256]{2,0,1:T(8,128)} async-done(((f32[512,8,256]{2,0,1:T(8,128)}), f32[512,8,256]{2,0,1:T(8,128)}, u32[]{:S(2)}, u32[]{:S(2)}) %all-to-all-start) | async-done | bytes 4194336 | tf_op jit(solution)/shard_map/all_to_all | solution.py:54
  106.2 0.0 copy-done
  106.2 0.0 copy-start.1
  106.2 194.2 %while.16 = (s32[]{:T(128)}, f32[256,2048]{1,0:T(8,128)S(1)}, f32[4096,256]{1,0:T(8,128)}, s32[2048]{0:T(1024)S(1)}, s32[]{:T(128)}, /*index=5*/s32[]{:T(128)}, s32[]{:T(128)}, s32[]{:T(128)}) while((s32[]{:T(128)}, f32[256,2048]{1,0:T(8,128)S(1)}, f32[4096,256]{1,0:T(8,128)}, s32[2048]{0:T(1024)S(1)}, s32[]{:T(128)}, ...), condition=%wide.region_1.0_spmd.clone, body=%wide.region_0.0_spmd.clone.sunk | while | flops 3257930240 | bytes 4751509 | solution.py:48
  106.3 24.2 %fusion.75 = f32[256,2048]{1,0:T(8,128)S(1)} fusion(f32[256,2048]{1,0:T(8,128)S(1)} %get-tuple-element.179, s32[512]{0:T(512)S(1)} %get-tuple-element.168, s32[512]{0:T(512)S(1)} %get-tuple-element.169, s32[2048]{0:T(1024)S(1)} %broadcast_multiply_fusion.4, pred[]{:T(512)S(6)} %compare.3, f32[4096,256]{1,0:T(8,128)} %get-tuple-element.188, ...), kind=kOutput, calls=%fused_computation.36.clone.1 | convolution fusion | flops 3257925632 | bytes 4730885 | tf_op jit(solution)/shard_map/while/body/eval_jaxpr/dot_general | solution.py:40
  130.5 24.2 %fusion.75 = f32[256,2048]{1,0:T(8,128)S(1)} fusion(f32[256,2048]{1,0:T(8,128)S(1)} %get-tuple-element.179, s32[512]{0:T(512)S(1)} %get-tuple-element.168, s32[512]{0:T(512)S(1)} %get-tuple-element.169, s32[2048]{0:T(1024)S(1)} %broadcast_multiply_fusion.4, pred[]{:T(512)S(6)} %compare.3, f32[4096,256]{1,0:T(8,128)} %get-tuple-element.188, ...), kind=kOutput, calls=%fused_computation.36.clone.1 | convolution fusion | flops 3257925632 | bytes 4730885 | tf_op jit(solution)/shard_map/while/body/eval_jaxpr/dot_general | solution.py:40
  154.8 24.2 %fusion.75 = f32[256,2048]{1,0:T(8,128)S(1)} fusion(f32[256,2048]{1,0:T(8,128)S(1)} %get-tuple-element.179, s32[512]{0:T(512)S(1)} %get-tuple-element.168, s32[512]{0:T(512)S(1)} %get-tuple-element.169, s32[2048]{0:T(1024)S(1)} %broadcast_multiply_fusion.4, pred[]{:T(512)S(6)} %compare.3, f32[4096,256]{1,0:T(8,128)} %get-tuple-element.188, ...), kind=kOutput, calls=%fused_computation.36.clone.1 | convolution fusion | flops 3257925632 | bytes 4730885 | tf_op jit(solution)/shard_map/while/body/eval_jaxpr/dot_general | solution.py:40
  179.1 24.2 %fusion.75 = f32[256,2048]{1,0:T(8,128)S(1)} fusion(f32[256,2048]{1,0:T(8,128)S(1)} %get-tuple-element.179, s32[512]{0:T(512)S(1)} %get-tuple-element.168, s32[512]{0:T(512)S(1)} %get-tuple-element.169, s32[2048]{0:T(1024)S(1)} %broadcast_multiply_fusion.4, pred[]{:T(512)S(6)} %compare.3, f32[4096,256]{1,0:T(8,128)} %get-tuple-element.188, ...), kind=kOutput, calls=%fused_computation.36.clone.1 | convolution fusion | flops 3257925632 | bytes 4730885 | tf_op jit(solution)/shard_map/while/body/eval_jaxpr/dot_general | solution.py:40
  203.4 24.2 %fusion.75 = f32[256,2048]{1,0:T(8,128)S(1)} fusion(f32[256,2048]{1,0:T(8,128)S(1)} %get-tuple-element.179, s32[512]{0:T(512)S(1)} %get-tuple-element.168, s32[512]{0:T(512)S(1)} %get-tuple-element.169, s32[2048]{0:T(1024)S(1)} %broadcast_multiply_fusion.4, pred[]{:T(512)S(6)} %compare.3, f32[4096,256]{1,0:T(8,128)} %get-tuple-element.188, ...), kind=kOutput, calls=%fused_computation.36.clone.1 | convolution fusion | flops 3257925632 | bytes 4730885 | tf_op jit(solution)/shard_map/while/body/eval_jaxpr/dot_general | solution.py:40
  227.6 24.2 %fusion.75 = f32[256,2048]{1,0:T(8,128)S(1)} fusion(f32[256,2048]{1,0:T(8,128)S(1)} %get-tuple-element.179, s32[512]{0:T(512)S(1)} %get-tuple-element.168, s32[512]{0:T(512)S(1)} %get-tuple-element.169, s32[2048]{0:T(1024)S(1)} %broadcast_multiply_fusion.4, pred[]{:T(512)S(6)} %compare.3, f32[4096,256]{1,0:T(8,128)} %get-tuple-element.188, ...), kind=kOutput, calls=%fused_computation.36.clone.1 | convolution fusion | flops 3257925632 | bytes 4730885 | tf_op jit(solution)/shard_map/while/body/eval_jaxpr/dot_general | solution.py:40
  251.9 24.2 %fusion.75 = f32[256,2048]{1,0:T(8,128)S(1)} fusion(f32[256,2048]{1,0:T(8,128)S(1)} %get-tuple-element.179, s32[512]{0:T(512)S(1)} %get-tuple-element.168, s32[512]{0:T(512)S(1)} %get-tuple-element.169, s32[2048]{0:T(1024)S(1)} %broadcast_multiply_fusion.4, pred[]{:T(512)S(6)} %compare.3, f32[4096,256]{1,0:T(8,128)} %get-tuple-element.188, ...), kind=kOutput, calls=%fused_computation.36.clone.1 | convolution fusion | flops 3257925632 | bytes 4730885 | tf_op jit(solution)/shard_map/while/body/eval_jaxpr/dot_general | solution.py:40
  276.2 24.2 %fusion.75 = f32[256,2048]{1,0:T(8,128)S(1)} fusion(f32[256,2048]{1,0:T(8,128)S(1)} %get-tuple-element.179, s32[512]{0:T(512)S(1)} %get-tuple-element.168, s32[512]{0:T(512)S(1)} %get-tuple-element.169, s32[2048]{0:T(1024)S(1)} %broadcast_multiply_fusion.4, pred[]{:T(512)S(6)} %compare.3, f32[4096,256]{1,0:T(8,128)} %get-tuple-element.188, ...), kind=kOutput, calls=%fused_computation.36.clone.1 | convolution fusion | flops 3257925632 | bytes 4730885 | tf_op jit(solution)/shard_map/while/body/eval_jaxpr/dot_general | solution.py:40
  300.4 0.0 copy-done.1
  300.4 1.7 fusion.69
  302.1 32.0 %psum.7 = f32[2048]{0:T(1024)S(1)} all-reduce(f32[2048]{0:T(1024)S(1)} %get-tuple-element.137), channel_id=1, replica_groups=mesh['grp'=2,'mode'=8,'node'=2] {'mode','node'}, use_global_device_ids=true, to_apply=%region_3.0 | all-reduce | flops 2048 | bytes 16384 | tf_op jit(solution)/shard_map/psum | solution.py:57
  334.1 0.6 broadcast_multiply_fusion.2
  (17 shorter events, 0.1 us)
Async XLA Ops:
  5.5 100.7 %copy-start = (s32[2048]{0:T(1024)S(1)}, s32[2048]{0:T(1024)}, u32[]{:S(2)}) copy-start(s32[2048]{0:T(1024)} %param.9) | copy-start | bytes 24580
  5.5 100.7 %all-to-all-start = ((f32[512,8,256]{2,0,1:T(8,128)}), f32[512,8,256]{2,0,1:T(8,128)}, u32[]{:S(2)}, u32[]{:S(2)}) async-start(f32[512,8,256]{2,0,1:T(8,128)} %bitcast.8), calls=%async_computation | async-start | bytes 8388608 | tf_op jit(solution)/shard_map/all_to_all | solution.py:54
  106.2 194.2 %copy-start.1 = (f32[256]{0:T(256)S(1)}, f32[256]{0:T(256)}, u32[]{:S(2)}) copy-start(f32[256]{0:T(256)} %param.8) | copy-start | bytes 3076
where the time goes:
time: 335 us
  matrix products  194 us (58%)
  waiting for transfers between devices  93.3 us (28%)
  blocking collectives  32 us (10%)
  starting transfers between devices  7.41 us (2%)
  other arithmetic  4.88 us (1%)
    dot_general x8, matrix products, add_block(): lax.dot_general(rows, coeffs, (((0,), (0,)), ((), ())), precision=lax.Pre...  194 us
    all_to_all x1, waiting for transfers between devices, on_device(): lax.all_to_all(scaled, 'mode', split_axis=1, concat_axis=0, tiled=True)  93.3 us
    psum x1, blocking collectives, on_device(): totals = lax.psum(jnp.sum(modulus, axis=0), ('mode', 'node'))  32 us
    all_to_all x1, starting transfers between devices, on_device(): lax.all_to_all(scaled, 'mode', split_axis=1, concat_axis=0, tiled=True)  7.41 us
  transfers between devices with their start and end apart: 1, of which 1 were waited for; matrix products, arithmetic and copies ran while one was open for 0% of the time, Pallas kernels for 0%

commit v1 on v0

--- a/solution.py
+++ b/solution.py
@@ -54,7 +54,8 @@
     gathered = lax.all_to_all(scaled, "mode", split_axis=1, concat_axis=0, tiled=True)
     summed = contract_all(gathered, sample_seeds)
     modulus = jnp.exp(mean_log[:, None] + summed)
-    totals = lax.psum(jnp.sum(modulus, axis=0), ("mode", "node"))
+    write_view_up = lambda inner_x, ax_name: jnp.sum(jax.lax.all_gather(inner_x, ax_name), axis=0)
+    totals = write_view_up(jnp.sum(modulus, axis=0), ax_name=("mode", "node"))
     node_count = own_rows * lax.axis_size("mode") * lax.axis_size("node")
     return (modulus, totals / node_count)
 

time: 335 us -> 323 us (0.964)
  blocking collectives: 32 us -> 19.8 us
    psum x1 -> x0, blocking collectives: 32 us -> none  [on_device(): totals = lax.psum(jnp.sum(modulus, axis=0), ('mode', 'node'))]
    all_gather x0 -> x1, blocking collectives: none -> 19.8 us  [on_device(): jax.lax.all_gather(inner_x, ax_name)]
where the time goes in v1:
time: 323 us
  matrix products  194 us (60%)
  waiting for transfers between devices  93.3 us (29%)
  blocking collectives  19.8 us (6%)
  starting transfers between devices  7.41 us (2%)
  other arithmetic  4.9 us (2%)
    dot_general x8, matrix products, add_block(): lax.dot_general(rows, coeffs, (((0,), (0,)), ((), ())), precision=lax.Pre...  194 us
    all_to_all x1, waiting for transfers between devices, on_device(): lax.all_to_all(scaled, 'mode', split_axis=1, concat_axis=0, tiled=True)  93.3 us
    all_gather x1, blocking collectives, on_device(): jax.lax.all_gather(inner_x, ax_name)  19.8 us
    all_to_all x1, starting transfers between devices, on_device(): lax.all_to_all(scaled, 'mode', split_axis=1, concat_axis=0, tiled=True)  7.41 us
  transfers between devices with their start and end apart: 1, of which 1 were waited for; matrix products, arithmetic and copies ran while one was open for 0% of the time, Pallas kernels for 0%

profile of v1, /device:TPU:0, one launch (start us, length us, event | category | flops | bytes accessed | tf_op | source)
XLA Modules:
  0.0 322.6 jit_solution(9304988573078148034)
XLA Ops:
  0.6 2.5 broadcast_multiply_fusion.1
  3.2 2.4 copy.11
  5.5 0.0 copy-start
  5.5 7.4 %all-to-all-start = ((f32[512,8,256]{2,0,1:T(8,128)}), f32[512,8,256]{2,0,1:T(8,128)}, u32[]{:S(2)}, u32[]{:S(2)}) async-start(f32[512,8,256]{2,0,1:T(8,128)} %bitcast.8), calls=%async_computation | async-start | bytes 8388608 | tf_op jit(solution)/shard_map/all_to_all | solution.py:54
  12.9 93.3 %all-to-all-done = f32[512,8,256]{2,0,1:T(8,128)} async-done(((f32[512,8,256]{2,0,1:T(8,128)}), f32[512,8,256]{2,0,1:T(8,128)}, u32[]{:S(2)}, u32[]{:S(2)}) %all-to-all-start) | async-done | bytes 4194336 | tf_op jit(solution)/shard_map/all_to_all | solution.py:54
  106.2 0.0 copy-done
  106.2 0.0 copy-start.1
  106.2 194.2 %while.16 = (s32[]{:T(128)}, f32[256,2048]{1,0:T(8,128)S(1)}, f32[4096,256]{1,0:T(8,128)}, s32[2048]{0:T(1024)S(1)}, s32[]{:T(128)}, /*index=5*/s32[]{:T(128)}, s32[]{:T(128)}, s32[]{:T(128)}) while((s32[]{:T(128)}, f32[256,2048]{1,0:T(8,128)S(1)}, f32[4096,256]{1,0:T(8,128)}, s32[2048]{0:T(1024)S(1)}, s32[]{:T(128)}, ...), condition=%wide.region_1.0_spmd.clone, body=%wide.region_0.0_spmd.clone.sunk | while | flops 3257930240 | bytes 4751509 | solution.py:48
  106.3 24.2 %fusion.75 = f32[256,2048]{1,0:T(8,128)S(1)} fusion(f32[256,2048]{1,0:T(8,128)S(1)} %get-tuple-element.179, s32[512]{0:T(512)S(1)} %get-tuple-element.168, s32[512]{0:T(512)S(1)} %get-tuple-element.169, s32[2048]{0:T(1024)S(1)} %broadcast_multiply_fusion.4, pred[]{:T(512)S(6)} %compare.3, f32[4096,256]{1,0:T(8,128)} %get-tuple-element.188, ...), kind=kOutput, calls=%fused_computation.36.clone.1 | convolution fusion | flops 3257925632 | bytes 4730885 | tf_op jit(solution)/shard_map/while/body/eval_jaxpr/dot_general | solution.py:40
  130.5 24.2 %fusion.75 = f32[256,2048]{1,0:T(8,128)S(1)} fusion(f32[256,2048]{1,0:T(8,128)S(1)} %get-tuple-element.179, s32[512]{0:T(512)S(1)} %get-tuple-element.168, s32[512]{0:T(512)S(1)} %get-tuple-element.169, s32[2048]{0:T(1024)S(1)} %broadcast_multiply_fusion.4, pred[]{:T(512)S(6)} %compare.3, f32[4096,256]{1,0:T(8,128)} %get-tuple-element.188, ...), kind=kOutput, calls=%fused_computation.36.clone.1 | convolution fusion | flops 3257925632 | bytes 4730885 | tf_op jit(solution)/shard_map/while/body/eval_jaxpr/dot_general | solution.py:40
  154.8 24.2 %fusion.75 = f32[256,2048]{1,0:T(8,128)S(1)} fusion(f32[256,2048]{1,0:T(8,128)S(1)} %get-tuple-element.179, s32[512]{0:T(512)S(1)} %get-tuple-element.168, s32[512]{0:T(512)S(1)} %get-tuple-element.169, s32[2048]{0:T(1024)S(1)} %broadcast_multiply_fusion.4, pred[]{:T(512)S(6)} %compare.3, f32[4096,256]{1,0:T(8,128)} %get-tuple-element.188, ...), kind=kOutput, calls=%fused_computation.36.clone.1 | convolution fusion | flops 3257925632 | bytes 4730885 | tf_op jit(solution)/shard_map/while/body/eval_jaxpr/dot_general | solution.py:40
  179.1 24.2 %fusion.75 = f32[256,2048]{1,0:T(8,128)S(1)} fusion(f32[256,2048]{1,0:T(8,128)S(1)} %get-tuple-element.179, s32[512]{0:T(512)S(1)} %get-tuple-element.168, s32[512]{0:T(512)S(1)} %get-tuple-element.169, s32[2048]{0:T(1024)S(1)} %broadcast_multiply_fusion.4, pred[]{:T(512)S(6)} %compare.3, f32[4096,256]{1,0:T(8,128)} %get-tuple-element.188, ...), kind=kOutput, calls=%fused_computation.36.clone.1 | convolution fusion | flops 3257925632 | bytes 4730885 | tf_op jit(solution)/shard_map/while/body/eval_jaxpr/dot_general | solution.py:40
  203.4 24.2 %fusion.75 = f32[256,2048]{1,0:T(8,128)S(1)} fusion(f32[256,2048]{1,0:T(8,128)S(1)} %get-tuple-element.179, s32[512]{0:T(512)S(1)} %get-tuple-element.168, s32[512]{0:T(512)S(1)} %get-tuple-element.169, s32[2048]{0:T(1024)S(1)} %broadcast_multiply_fusion.4, pred[]{:T(512)S(6)} %compare.3, f32[4096,256]{1,0:T(8,128)} %get-tuple-element.188, ...), kind=kOutput, calls=%fused_computation.36.clone.1 | convolution fusion | flops 3257925632 | bytes 4730885 | tf_op jit(solution)/shard_map/while/body/eval_jaxpr/dot_general | solution.py:40
  227.6 24.2 %fusion.75 = f32[256,2048]{1,0:T(8,128)S(1)} fusion(f32[256,2048]{1,0:T(8,128)S(1)} %get-tuple-element.179, s32[512]{0:T(512)S(1)} %get-tuple-element.168, s32[512]{0:T(512)S(1)} %get-tuple-element.169, s32[2048]{0:T(1024)S(1)} %broadcast_multiply_fusion.4, pred[]{:T(512)S(6)} %compare.3, f32[4096,256]{1,0:T(8,128)} %get-tuple-element.188, ...), kind=kOutput, calls=%fused_computation.36.clone.1 | convolution fusion | flops 3257925632 | bytes 4730885 | tf_op jit(solution)/shard_map/while/body/eval_jaxpr/dot_general | solution.py:40
  251.9 24.2 %fusion.75 = f32[256,2048]{1,0:T(8,128)S(1)} fusion(f32[256,2048]{1,0:T(8,128)S(1)} %get-tuple-element.179, s32[512]{0:T(512)S(1)} %get-tuple-element.168, s32[512]{0:T(512)S(1)} %get-tuple-element.169, s32[2048]{0:T(1024)S(1)} %broadcast_multiply_fusion.4, pred[]{:T(512)S(6)} %compare.3, f32[4096,256]{1,0:T(8,128)} %get-tuple-element.188, ...), kind=kOutput, calls=%fused_computation.36.clone.1 | convolution fusion | flops 3257925632 | bytes 4730885 | tf_op jit(solution)/shard_map/while/body/eval_jaxpr/dot_general | solution.py:40
  276.2 24.2 %fusion.75 = f32[256,2048]{1,0:T(8,128)S(1)} fusion(f32[256,2048]{1,0:T(8,128)S(1)} %get-tuple-element.179, s32[512]{0:T(512)S(1)} %get-tuple-element.168, s32[512]{0:T(512)S(1)} %get-tuple-element.169, s32[2048]{0:T(1024)S(1)} %broadcast_multiply_fusion.4, pred[]{:T(512)S(6)} %compare.3, f32[4096,256]{1,0:T(8,128)} %get-tuple-element.188, ...), kind=kOutput, calls=%fused_computation.36.clone.1 | convolution fusion | flops 3257925632 | bytes 4730885 | tf_op jit(solution)/shard_map/while/body/eval_jaxpr/dot_general | solution.py:40
  300.4 0.0 copy-done.1
  300.4 1.7 fusion.69
  302.1 19.8 %all-gather = f32[32768]{0:T(1024)S(1)} all-gather(f32[2048]{0:T(1024)S(1)} %get-tuple-element.137), channel_id=2, replica_groups=mesh['grp'=2,'mode'=8,'node'=2] {'mode','node'}, dimensions={0}, use_global_device_ids=true | all-gather | bytes 139264 | tf_op jit(solution)/shard_map/all_gather | solution.py:57
  322.0 0.6 broadcast_multiply_fusion.2
  (19 shorter events, 0.1 us)
Async XLA Ops:
  5.5 100.7 %copy-start = (s32[2048]{0:T(1024)S(1)}, s32[2048]{0:T(1024)}, u32[]{:S(2)}) copy-start(s32[2048]{0:T(1024)} %param.9) | copy-start | bytes 24580
  5.5 100.7 %all-to-all-start = ((f32[512,8,256]{2,0,1:T(8,128)}), f32[512,8,256]{2,0,1:T(8,128)}, u32[]{:S(2)}, u32[]{:S(2)}) async-start(f32[512,8,256]{2,0,1:T(8,128)} %bitcast.8), calls=%async_computation | async-start | bytes 8388608 | tf_op jit(solution)/shard_map/all_to_all | solution.py:54
  106.2 194.2 %copy-start.1 = (f32[256]{0:T(256)S(1)}, f32[256]{0:T(256)}, u32[]{:S(2)}) copy-start(f32[256]{0:T(256)} %param.8) | copy-start | bytes 3076
